TPU v7x, 128 devices: a whole 4x4x4 slice. The times are simulated.
128 devices in a mesh: fsdp: 16 (over y_hi, z, core), tensor: 8 (over y_lo, x).
Axes of the slice: x: 4, y: 4 (y_hi: 2, y_lo: 2; y = y_hi * 2 + y_lo), z: 4, core: 2. Of those that a mesh axis runs over, the one named last changes fastest.
Arguments:
- states: bfloat16 [4096, 8192], P('fsdp'), may hold values from -64 to 64
- segment_ids: int32 [16, 256], P('fsdp'), may hold values from 0 to 3, never falling along the last dimension, each value on 1 to 128 neighbouring positions
- attn_gain: float32 [8192], replicated, may hold values from 0.1 to 1.9
- query_weight: bfloat16 [8192, 4096], P('fsdp', 'tensor'), may hold values from -2 to 2
- key_weight: bfloat16 [8192, 1024], P('fsdp', 'tensor'), may hold values from -2 to 2
- value_matrix: bfloat16 [8192, 1024], P('fsdp', 'tensor'), may hold values from -0.0625 to 0.0625
- out_weight: bfloat16 [4096, 8192], P('tensor', 'fsdp'), may hold values from -0.28125 to 0.28125
- final_gain: float32 [8192], P('tensor'), may hold values from 0.1 to 1.9
- head_weight: float32 [8192], P('tensor'), may hold values from -0.0625 to 0.0625
Outputs:
- scores: float32 [4096], P(('fsdp', 'tensor'))
- resid_out: bfloat16 [4096, 8192], P('fsdp', 'tensor')
Inputs may be any that keep to these rules, and one draw needn't show every extreme that they name: `segment_ids`: in each row, segment numbers never fall and each rollout spans 1 to 128 positions.
All inputs are finite; a program needn't handle non-finite values.
Results may differ from a plain program's by a relative error of at most 0.0071.
Values may be sent and summed in bfloat16 or wider, within the bound.
A program may use at most 128 MiB of HBM per device.

v0:
```python
import jax
import jax.numpy as jnp
from jax import lax
from jax.sharding import PartitionSpec as P

MODEL_WIDTH = 8192
HEAD_SIZE = 128
EPS = 1e-05
THETA = 500000.0
NEG_FILL = -1e30


def in_one_piece(arrays, axis, dim, along):
    both = jnp.concatenate(arrays, axis=along)
    result, at, outs = (lax.all_gather(both, axis, axis=dim, tiled=True), 0, [])
    for a in arrays:
        outs.append(lax.slice_in_dim(result, at, at + a.shape[along], axis=along))
        at += a.shape[along]
    return tuple(outs)


def sent_to_all(value, axis):
    length = lax.axis_size(axis)
    return lax.all_to_all(
        jnp.broadcast_to(value[None], (length, *value.shape)), axis, 0, 0, tiled=True
    )


def over_copies(value, axis):
    return sent_to_all(value, axis).sum(axis=0)


def together(arrays, axis):
    ravelled, at, outs = (jnp.concatenate([a.reshape(-1) for a in arrays]), 0, [])
    total = over_copies(ravelled, axis)
    for a in arrays:
        outs.append(total[at : at + a.size].reshape(a.shape))
        at += a.size
    return tuple(outs)


def rope_tables(seg_row):
    count = seg_row.shape[0]
    places = jnp.arange(count, dtype=jnp.int32)
    boundary = jnp.concatenate([jnp.ones((1,), dtype=bool), seg_row[1:] != seg_row[:-1]])
    begins = lax.cummax(jnp.where(boundary, places, jnp.zeros_like(places)), axis=0)
    positions = (places - begins).astype(jnp.float32)
    half_width = HEAD_SIZE // 2
    frequency = THETA ** (-(2.0 * jnp.arange(half_width, dtype=jnp.float32)) / HEAD_SIZE)
    angles = positions[:, None] * frequency[None, :]
    return (jnp.cos(angles), jnp.sin(angles))


def rotated(block, cosine, sine_part):
    half_width = block.shape[-1] // 2
    first_half = block[..., :half_width]
    second_half = block[..., half_width:]
    cos_rows = cosine[:, None, :]
    sin_rows = sine_part[:, None, :]
    return jnp.concatenate(
        [
            first_half * cos_rows - second_half * sin_rows,
            second_half * cos_rows + first_half * sin_rows,
        ],
        axis=-1,
    )


def attend(queries, key_rows, values, seg_row):
    t_rows = queries.shape[0]
    heads_here = queries.shape[1] // HEAD_SIZE
    groups_here = key_rows.shape[1] // HEAD_SIZE
    ratio = heads_here // groups_here
    cosine, sine_part = rope_tables(seg_row)
    query_rot = rotated(queries.reshape(t_rows, heads_here, HEAD_SIZE), cosine, sine_part).astype(
        jnp.bfloat16
    )
    key_rot = rotated(key_rows.reshape(t_rows, groups_here, HEAD_SIZE), cosine, sine_part).astype(
        jnp.bfloat16
    )
    value_rows = values.astype(jnp.bfloat16).reshape(t_rows, groups_here, HEAD_SIZE)
    grouped = query_rot.reshape(t_rows, groups_here, ratio, HEAD_SIZE)
    logits = jnp.einsum(
        "tkgd,skd->kgts", grouped, key_rot, preferred_element_type=jnp.float32
    ) * HEAD_SIZE ** (-0.5)
    places = jnp.arange(t_rows, dtype=jnp.int32)
    allowed = (seg_row[:, None] == seg_row[None, :]) & (places[None, :] <= places[:, None])
    logits = jnp.where(allowed[None, None], logits, NEG_FILL)
    row_peak = jnp.max(logits, axis=-1, keepdims=True)
    raised = jnp.exp(logits - row_peak)
    probabilities = (raised / jnp.sum(raised, axis=-1, keepdims=True)).astype(jnp.bfloat16)
    mixed = jnp.einsum(
        "kgts,skd->tkgd", probabilities, value_rows, preferred_element_type=jnp.float32
    )
    return mixed.astype(jnp.bfloat16).reshape(t_rows, heads_here * HEAD_SIZE)


def body(
    states,
    segment_ids,
    attn_gain,
    query_weight,
    key_weight,
    value_matrix,
    out_weight,
    final_gain,
    head_weight,
):
    t_rows, width = states.shape
    tensor_count = lax.axis_size("tensor")
    tensor_index = lax.axis_index("tensor")
    widened = states.astype(jnp.float32)
    normed = (
        widened
        * lax.rsqrt(jnp.sum(widened * widened, axis=1, keepdims=True) / MODEL_WIDTH + EPS)
        * attn_gain[None, :]
    ).astype(jnp.bfloat16)

    def add_piece(portion):
        return jnp.dot(normed, portion, preferred_element_type=jnp.float32)

    pieces = in_one_piece((query_weight, key_weight, value_matrix), "fsdp", 0, 1)
    queries = add_piece(pieces[0])
    key_rows = add_piece(pieces[1])
    values = add_piece(pieces[2])
    mixed = attend(queries, key_rows, values, segment_ids[0])
    slice_cols = width // tensor_count
    partials = jnp.dot(
        mixed,
        lax.all_gather(out_weight, "fsdp", axis=1, tiled=True),
        preferred_element_type=jnp.float32,
    )
    branch = lax.psum_scatter(partials, "tensor", scatter_dimension=1, tiled=True)
    own_cols = lax.dynamic_slice_in_dim(widened, tensor_index * slice_cols, slice_cols, 1)
    resid_out = (own_cols + branch).astype(jnp.bfloat16)
    stream = resid_out.astype(jnp.float32)
    squares = jnp.sum(stream * stream, axis=1)
    products = jnp.sum(stream * (final_gain * head_weight)[None, :], axis=1)
    share_rows = t_rows // tensor_count
    squares_all, products_all = together((squares, products), "tensor")
    local_squares = lax.dynamic_slice_in_dim(squares_all, tensor_index * share_rows, share_rows, 0)
    products_mine = lax.dynamic_slice_in_dim(products_all, tensor_index * share_rows, share_rows, 0)
    scores = products_mine * lax.rsqrt(local_squares / MODEL_WIDTH + EPS)
    return (scores, resid_out)


def solution(mesh):
    placed = (
        P("fsdp", None),
        P("fsdp", None),
        P(),
        P("fsdp", "tensor"),
        P("fsdp", "tensor"),
        P("fsdp", "tensor"),
        P("tensor", "fsdp"),
        P("tensor"),
        P("tensor"),
    )
    return jax.shard_map(
        body,
        mesh=mesh,
        in_specs=placed,
        out_specs=(P(("fsdp", "tensor")), P("fsdp", "tensor")),
        check_vma=False,
    )
```

profile of v0, /device:TPU:0, one launch (start us, length us, event | category | flops | bytes accessed | tf_op | source)
XLA Modules:
  0.0 299.0 jit_solution(9830881361931489665)
XLA Ops:
  7.2 2.1 pad_maximum_fusion
  9.4 0.0 all-gather.5.cloned.1.call-start
  9.4 0.7 all-gather.5.cloned.1.call-update
  10.1 0.0 reduce-scatter.2.cloned.1.call-start
  10.2 0.8 compare_reduce_fusion
  11.0 0.1 fusion.40
  11.1 0.3 reduce-window.9
  11.4 0.1 slice.47
  11.5 0.1 slice_reduce_fusion
  11.6 3.1 %multiply_reduce_fusion = f32[256]{0:T(256)S(1)} fusion(bf16[256,8192]{1,0:T(8,128)(2,1)} %param.9), kind=kLoop, calls=%fused_computation.3 | loop fusion | flops 6291200 | bytes 4195328 | tf_op jit(solution)/shard_map/reduce_sum | solution.py:115
  14.8 0.1 fusion.41
  14.8 0.9 fusion.27
  15.7 0.5 multiply_cosine_fusion
  16.2 87.3 %all-gather.3.cloned.1.call-done = bf16[8192,768]{1,0:T(8,128)(2,1)} async-done(((bf16[512,768]{1,0:T(8,128)(2,1)}), bf16[8192,768]{1,0:T(8,128)(2,1)}) %all-gather.3.cloned.1.call-update) | async-done | bytes 12582928 | tf_op jit(solution)/shard_map/all_gather | solution.py:15
  103.6 7.1 %fusion = f32[256,512]{1,0:T(8,128)S(1)} fusion(bf16[8192,768]{1,0:T(8,128)(2,1)} %all-gather.3.cloned.1.call-done, f32[8192]{0:T(1024)} %param.11, f32[256]{0:T(256)S(1)} %add_rsqrt_fusion, bf16[256,8192]{1,0:T(8,128)(2,1)} %param.9), kind=kOutput, calls=%fused_computation | convolution fusion | flops 2155872256 | bytes 13140992 | tf_op jit(solution)/shard_map/dot_general | solution.py:120
  110.6 0.2 reshape.251
  110.8 4.9 %fusion.8 = f32[256,1,128]{0,2,1:T(8,128)S(1)} fusion(bf16[8192,768]{1,0:T(8,128)(2,1)} %all-gather.3.cloned.1.call-done, f32[8192]{0:T(1024)S(1)} %copy-done.2, f32[256]{0:T(256)S(1)} %add_rsqrt_fusion, bf16[256,8192]{1,0:T(8,128)(2,1)} %param.9), kind=kOutput, calls=%fused_computation.14 | convolution fusion | flops 545259520 | bytes 6456320 | tf_op jit(solution)/shard_map/dot_general | solution.py:120
  115.7 0.3 fusion.39
  116.0 0.3 fusion.43
  116.4 0.1 subtract_convert_fusion
  116.5 0.4 fusion.45
  117.0 0.2 fusion.21
  117.1 4.6 %convolution_convert_fusion = bf16[128,4,256]{2,0,1:T(8,128)(2,1)S(1)} fusion(bf16[8192,768]{1,0:T(8,128)(2,1)} %all-gather.3.cloned.1.call-done, f32[1,4,256,256]{2,3,1,0:T(8,128)S(1)} %get-tuple-element.16, f32[4,256]{1,0:T(4,128)S(1)} %fusion.21, f32[4,256]{1,0:T(4,128)S(1)} %get-tuple-element.15, f32[8192]{0:T(1024)S(1)} %copy-done.2, ...), kind=kOutput, calls=%fused_computation.13 | convolution fusion | flops 613318656 | bytes 7644160 | tf_op jit(solution)/shard_map/kgts,skd->tkgd/dot_general | solution.py:92
  121.7 58.3 %all-gather.5.cloned.1.call-done = bf16[512,8192]{1,0:T(8,128)(2,1)} async-done(((bf16[512,512]{1,0:T(8,128)(2,1)}), bf16[512,8192]{1,0:T(8,128)(2,1)}) %all-gather.5.cloned.1.call-update) | async-done | bytes 8388624 | tf_op jit(solution)/shard_map/all_gather | solution.py:130
  180.0 9.0 %fusion.46 = f32[256,8192]{1,0:T(8,128)} fusion(bf16[256,512]{0,1:T(8,128)(2,1)S(1)} %bitcast.40, bf16[512,8192]{1,0:T(8,128)(2,1)} %all-gather.5.cloned.1.call-done), kind=kOutput, calls=%fused_computation.64 | convolution fusion | flops 2147483648 | bytes 17039360 | tf_op jit(solution)/shard_map/dot_general | solution.py:128
  189.1 6.7 %convert_element_type.41 = f32[256,8192]{1,0:T(8,128)} convert(bf16[256,8192]{1,0:T(8,128)(2,1)} %param.9) | non-fusion elementwise | flops 2097152 | bytes 12582912 | tf_op jit(solution)/shard_map/convert_element_type | solution.py:112
  195.7 83.5 %reduce-scatter.2.cloned.1.call-done = f32[256,1024]{1,0:T(8,128)} async-done(((f32[256,8192]{1,0:T(8,128)}), f32[256,1024]{1,0:T(8,128)}) %reduce-scatter.2.cloned.1.call-update) | async-done | bytes 1048592 | tf_op jit(solution)/shard_map/reduce_scatter | solution.py:133
  279.2 2.5 fusion.19
  281.8 0.6 broadcast_in_dim.15
  282.4 3.3 %all-to-all-start = ((f32[8,1,512]{2,1,0:T(1,128)}), f32[8,1,512]{2,1,0:T(1,128)S(1)}, u32[]{:S(2)}, u32[]{:S(2)}) async-start(f32[8,1,512]{2,1,0:T(1,128)} %broadcast_in_dim.15), calls=%async_computation.1 | async-start | bytes 32768 | tf_op jit(solution)/shard_map/all_to_all | solution.py:24
  285.7 6.1 %all-to-all-done = f32[8,1,512]{2,1,0:T(1,128)S(1)} async-done(((f32[8,1,512]{2,1,0:T(1,128)}), f32[8,1,512]{2,1,0:T(1,128)S(1)}, u32[]{:S(2)}, u32[]{:S(2)}) %all-to-all-start) | async-done | bytes 16416 | tf_op jit(solution)/shard_map/all_to_all | solution.py:24
  291.9 0.6 rsqrt_multiply_fusion
  (16 shorter events, 0.2 us)
Async XLA Ops:
  7.2 96.4 %all-gather.3.cloned.1.call-start = ((), (), s32[]{:S(2)}) async-start(), calls=%async_computation.2 | async-start | bytes 13369344 | tf_op jit(solution)/shard_map/all_gather | solution.py:15
  9.4 170.7 %all-gather.5.cloned.1.call-start = ((), (), s32[]{:S(2)}) async-start(), calls=%async_computation.3 | async-start | bytes 8912896 | tf_op jit(solution)/shard_map/all_gather | solution.py:130
  10.1 269.1 %reduce-scatter.2.cloned.1.call-start = ((), (), s32[]{:S(2)}) async-start(), calls=%async_computation.4 | async-start | bytes 9437184 | tf_op jit(solution)/shard_map/reduce_scatter | solution.py:133
  16.2 94.6 %copy-start.2 = (f32[8192]{0:T(1024)S(1)}, f32[8192]{0:T(1024)}, u32[]{:S(2)}) copy-start(f32[8192]{0:T(1024)} %param.11) | copy-start | bytes 98308
  189.0 6.7 %copy-start = (f32[1024]{0:T(1024)S(1)}, f32[1024]{0:T(1024)}, u32[]{:S(2)}) copy-start(f32[1024]{0:T(1024)} %param.16) | copy-start | bytes 12292
  189.1 6.7 %copy-start.1 = (f32[1024]{0:T(1024)S(1)}, f32[1024]{0:T(1024)}, u32[]{:S(2)}) copy-start(f32[1024]{0:T(1024)} %param.17) | copy-start | bytes 12292
  282.4 9.5 %all-to-all-start = ((f32[8,1,512]{2,1,0:T(1,128)}), f32[8,1,512]{2,1,0:T(1,128)S(1)}, u32[]{:S(2)}, u32[]{:S(2)}) async-start(f32[8,1,512]{2,1,0:T(1,128)} %broadcast_in_dim.15), calls=%async_computation.1 | async-start | bytes 32768 | tf_op jit(solution)/shard_map/all_to_all | solution.py:24
Sparse Core Ops, SparseCore 0:
  10.5 93.0 all-gather.2
  105.8 74.1 all-gather.4
  189.2 90.0 reduce-scatter.1
where the time goes:
time: 299 us
  waiting for transfers between devices  236 us (79%)
  matrix products  25.9 us (9%)
  other arithmetic  18.4 us (6%)
  between operations  13.9 us (5%)
  starting transfers between devices  3.45 us (1%)
    all_gather x1, waiting for transfers between devices, in_one_piece(): result, at, outs = (lax.all_gather(both, axis, axis=dim, tiled=True), 0, [])  87.3 us
    reduce_scatter x1, waiting for transfers between devices, body(): lax.psum_scatter(partials, 'tensor', scatter_dimension=1, tiled=True)  83.5 us
    all_gather x1, waiting for transfers between devices, body(): lax.all_gather(out_weight, 'fsdp', axis=1, tiled=True)  58.3 us
    dot_general x2, matrix products, add_piece(): return jnp.dot(normed, portion, preferred_element_type=jnp.float32)  11.9 us
    dot_general x1, matrix products, body(): jnp.dot(mixed, lax.all_gather(out_weight, 'fsdp', axis=1, tiled=True), pr...  8.98 us
    convert_element_type x1, other arithmetic, body(): widened = states.astype(jnp.float32)  6.65 us
    all_to_all x1, waiting for transfers between devices, sent_to_all(): lax.all_to_all(jnp.broadcast_to(value[None], (length, *value.shape)), axi...  6.14 us
  transfers between devices with their start and end apart: 4, of which 4 were waited for; matrix products, arithmetic and copies ran while one was open for 10% of the time, Pallas kernels for 0%

commit v1 on v0

--- a/solution.py
+++ b/solution.py
@@ -1,3 +1,4 @@
+import functools
 import jax
 import jax.numpy as jnp
 from jax import lax
@@ -8,6 +9,13 @@
 EPS = 1e-05
 THETA = 500000.0
 NEG_FILL = -1e30
+
+
+def proceed_group(array_here, dim_no):
+    return jnp.concatenate(lax.all_gather(array_here, "fsdp"), axis=dim_no)
+
+
+test_runs = functools.partial(proceed_group, dim_no=1)
 
 
 def in_one_piece(arrays, axis, dim, along):
@@ -125,11 +133,7 @@
     values = add_piece(pieces[2])
     mixed = attend(queries, key_rows, values, segment_ids[0])
     slice_cols = width // tensor_count
-    partials = jnp.dot(
-        mixed,
-        lax.all_gather(out_weight, "fsdp", axis=1, tiled=True),
-        preferred_element_type=jnp.float32,
-    )
+    partials = jnp.dot(mixed, test_runs(out_weight), preferred_element_type=jnp.float32)
     branch = lax.psum_scatter(partials, "tensor", scatter_dimension=1, tiled=True)
     own_cols = lax.dynamic_slice_in_dim(widened, tensor_index * slice_cols, slice_cols, 1)
     resid_out = (own_cols + branch).astype(jnp.bfloat16)

time: 299 us -> 314 us (1.050)
  local copies, waits for them, and re-layouts: 1.34 us -> 13.7 us
    reshape x0 -> x1, local copies, waits for them, and re-layouts: none -> 12.3 us  [proceed_group(): return jnp.concatenate(lax.all_gather(array_here, 'fsdp'), axis=dim_no)]
    all_gather x1, waiting for transfers between devices: 58.3 us -> 69.5 us  [proceed_group(): return jnp.concatenate(lax.all_gather(array_here, 'fsdp'), axis=dim_no)]
    all_gather x1, waiting for transfers between devices: 87.3 us -> 78.4 us  [in_one_piece(): result, at, outs = (lax.all_gather(both, axis, axis=dim, tiled=True), 0, [])]
  transfers between devices with their start and end apart: 4 -> 4, of which waited for: 4 -> 4; matrix products, arithmetic and copies ran while one was open for 10% -> 9% of each run, Pallas kernels for 0% -> 0%
where the time goes in v1:
time: 314 us
  waiting for transfers between devices  239 us (76%)
  matrix products  25.7 us (8%)
  other arithmetic  18.3 us (6%)
  between operations  13.9 us (4%)
  local copies, waits for them, and re-layouts  13.7 us (4%)
  starting transfers between devices  3.45 us (1%)
    reduce_scatter x1, waiting for transfers between devices, body(): lax.psum_scatter(partials, 'tensor', scatter_dimension=1, tiled=True)  83.9 us
    all_gather x1, waiting for transfers between devices, in_one_piece(): result, at, outs = (lax.all_gather(both, axis, axis=dim, tiled=True), 0, [])  78.4 us
    all_gather x1, waiting for transfers between devices, proceed_group(): return jnp.concatenate(lax.all_gather(array_here, 'fsdp'), axis=dim_no)  69.5 us
    reshape x1, local copies, waits for them, and re-layouts, proceed_group(): return jnp.concatenate(lax.all_gather(array_here, 'fsdp'), axis=dim_no)  12.3 us
    dot_general x2, matrix products, add_piece(): return jnp.dot(normed, portion, preferred_element_type=jnp.float32)  11.7 us
    dot_general x1, matrix products, body(): jnp.dot(mixed, test_runs(out_weight), preferred_element_type=jnp.float32)  9.02 us
    convert_element_type x1, other arithmetic, body(): widened = states.astype(jnp.float32)  6.46 us
  transfers between devices with their start and end apart: 4, of which 4 were waited for; matrix products, arithmetic and copies ran while one was open for 9% of the time, Pallas kernels for 0%

profile of v1, /device:TPU:0, one launch (start us, length us, event | category | flops | bytes accessed | tf_op | source)
XLA Modules:
  0.0 313.6 jit_solution(18242430141904869723)
XLA Ops:
  7.2 0.7 all-gather.6.cloned.1.call-update
  7.9 2.2 pad_maximum_fusion
  10.1 0.0 reduce-scatter.2.cloned.1.call-start
  10.2 0.8 compare_reduce_fusion
  11.0 0.1 fusion.40
  11.1 0.3 reduce-window.9
  11.4 0.1 slice.47
  11.5 0.1 slice_reduce_fusion
  11.7 3.1 multiply_reduce_fusion
  14.8 0.1 fusion.41
  14.9 0.9 fusion.27
  15.7 0.5 multiply_cosine_fusion
  16.3 69.5 %all-gather.6.cloned.1.call-done = bf16[8192,512]{1,0:T(8,128)(2,1)} async-done(((bf16[512,512]{1,0:T(8,128)(2,1)}), bf16[8192,512]{1,0:T(8,128)(2,1)}) %all-gather.6.cloned.1.call-update) | async-done | bytes 8388624 | tf_op jit(solution)/shard_map/all_gather | solution.py:15
  85.8 12.3 %copy.36 = bf16[512,16,512]{0,2,1:T(8,128)(2,1)} copy(bf16[512,16,512]{2,0,1:T(8,128)(2,1)} %bitcast.45) | data formatting | bytes 16777216 | tf_op jit(solution)/shard_map/reshape | solution.py:15
  98.1 78.4 %all-gather.4.cloned.1.call-done = bf16[8192,768]{1,0:T(8,128)(2,1)} async-done(((bf16[512,768]{1,0:T(8,128)(2,1)}), bf16[8192,768]{1,0:T(8,128)(2,1)}) %all-gather.4.cloned.1.call-update) | async-done | bytes 12582928 | tf_op jit(solution)/shard_map/all_gather | solution.py:23
  176.6 7.0 %fusion = f32[256,512]{1,0:T(8,128)S(1)} fusion(bf16[8192,768]{1,0:T(8,128)(2,1)} %all-gather.4.cloned.1.call-done, f32[8192]{0:T(1024)S(1)} %copy-done.2, f32[256]{0:T(256)S(1)} %add_rsqrt_fusion, bf16[256,8192]{1,0:T(8,128)(2,1)} %param.9), kind=kOutput, calls=%fused_computation | convolution fusion | flops 2155872256 | bytes 13140992 | tf_op jit(solution)/shard_map/dot_general | solution.py:128
  183.6 0.2 reshape.257
  183.8 0.3 fusion.43
  184.1 4.6 %fusion.8 = f32[256,1,128]{0,2,1:T(8,128)S(1)} fusion(bf16[8192,768]{1,0:T(8,128)(2,1)} %all-gather.4.cloned.1.call-done, f32[8192]{0:T(1024)S(1)} %copy-done.2, f32[256]{0:T(256)S(1)} %add_rsqrt_fusion, bf16[256,8192]{1,0:T(8,128)(2,1)} %param.9), kind=kOutput, calls=%fused_computation.14 | convolution fusion | flops 545259520 | bytes 6456320 | tf_op jit(solution)/shard_map/dot_general | solution.py:128
  188.7 0.3 fusion.39
  189.1 0.1 subtract_convert_fusion
  189.2 0.4 fusion.45
  189.7 0.2 fusion.21
  189.8 4.6 %convolution_convert_fusion = bf16[128,4,256]{2,0,1:T(8,128)(2,1)S(1)} fusion(bf16[8192,768]{1,0:T(8,128)(2,1)} %all-gather.4.cloned.1.call-done, f32[1,4,256,256]{2,3,1,0:T(8,128)S(1)} %get-tuple-element.16, f32[4,256]{1,0:T(4,128)S(1)} %fusion.21, f32[4,256]{1,0:T(4,128)S(1)} %get-tuple-element.15, f32[8192]{0:T(1024)S(1)} %copy-done.2, ...), kind=kOutput, calls=%fused_computation.13 | convolution fusion | flops 613318656 | bytes 7644160 | tf_op jit(solution)/shard_map/kgts,skd->tkgd/dot_general | solution.py:100
  194.4 9.0 %fusion.46 = f32[256,8192]{1,0:T(8,128)} fusion(bf16[256,512]{0,1:T(8,128)(2,1)S(1)} %bitcast.46, bf16[512,8192]{0,1:T(8,128)(2,1)} %bitcast.44), kind=kOutput, calls=%fused_computation.64 | convolution fusion | flops 2147483648 | bytes 17039360 | tf_op jit(solution)/shard_map/dot_general | solution.py:136
  203.5 6.5 %convert_element_type.41 = f32[256,8192]{1,0:T(8,128)} convert(bf16[256,8192]{1,0:T(8,128)(2,1)} %param.9) | non-fusion elementwise | flops 2097152 | bytes 12582912 | tf_op jit(solution)/shard_map/convert_element_type | solution.py:120
  209.9 83.9 %reduce-scatter.2.cloned.1.call-done = f32[256,1024]{1,0:T(8,128)} async-done(((f32[256,8192]{1,0:T(8,128)}), f32[256,1024]{1,0:T(8,128)}) %reduce-scatter.2.cloned.1.call-update) | async-done | bytes 1048592 | tf_op jit(solution)/shard_map/reduce_scatter | solution.py:137
  293.8 2.5 fusion.19
  296.4 0.6 broadcast_in_dim.15
  297.0 3.3 %all-to-all-start = ((f32[8,1,512]{2,1,0:T(1,128)}), f32[8,1,512]{2,1,0:T(1,128)S(1)}, u32[]{:S(2)}, u32[]{:S(2)}) async-start(f32[8,1,512]{2,1,0:T(1,128)} %broadcast_in_dim.15), calls=%async_computation.1 | async-start | bytes 32768 | tf_op jit(solution)/shard_map/all_to_all | solution.py:32
  300.3 6.1 %all-to-all-done = f32[8,1,512]{2,1,0:T(1,128)S(1)} async-done(((f32[8,1,512]{2,1,0:T(1,128)}), f32[8,1,512]{2,1,0:T(1,128)S(1)}, u32[]{:S(2)}, u32[]{:S(2)}) %all-to-all-start) | async-done | bytes 16416 | tf_op jit(solution)/shard_map/all_to_all | solution.py:32
  306.5 0.6 rsqrt_multiply_fusion
  (17 shorter events, 0.2 us)
Async XLA Ops:
  7.2 78.6 %all-gather.6.cloned.1.call-start = ((), (), s32[]{:S(2)}) async-start(), calls=%async_computation.4 | async-start | bytes 8912896 | tf_op jit(solution)/shard_map/all_gather | solution.py:15
  7.9 168.6 %all-gather.4.cloned.1.call-start = ((), (), s32[]{:S(2)}) async-start(), calls=%async_computation.2 | async-start | bytes 13369344 | tf_op jit(solution)/shard_map/all_gather | solution.py:23
  10.1 283.7 %reduce-scatter.2.cloned.1.call-start = ((), (), s32[]{:S(2)}) async-start(), calls=%async_computation.3 | async-start | bytes 9437184 | tf_op jit(solution)/shard_map/reduce_scatter | solution.py:137
  85.8 90.8 %copy-start.2 = (f32[8192]{0:T(1024)S(1)}, f32[8192]{0:T(1024)}, u32[]{:S(2)}) copy-start(f32[8192]{0:T(1024)} %param.11) | copy-start | bytes 98308
  203.4 6.5 %copy-start = (f32[1024]{0:T(1024)S(1)}, f32[1024]{0:T(1024)}, u32[]{:S(2)}) copy-start(f32[1024]{0:T(1024)} %param.16) | copy-start | bytes 12292
  203.4 6.5 %copy-start.1 = (f32[1024]{0:T(1024)S(1)}, f32[1024]{0:T(1024)}, u32[]{:S(2)}) copy-start(f32[1024]{0:T(1024)} %param.17) | copy-start | bytes 12292
  297.0 9.5 %all-to-all-start = ((f32[8,1,512]{2,1,0:T(1,128)}), f32[8,1,512]{2,1,0:T(1,128)S(1)}, u32[]{:S(2)}, u32[]{:S(2)}) async-start(f32[8,1,512]{2,1,0:T(1,128)} %broadcast_in_dim.15), calls=%async_computation.1 | async-start | bytes 32768 | tf_op jit(solution)/shard_map/all_to_all | solution.py:32
Sparse Core Ops, SparseCore 0:
  10.4 75.3 all-gather.5
  88.3 88.2 all-gather.3
  203.6 90.2 reduce-scatter.1
